TPU v7x, 32 devices: a whole 2x2x4 slice. The times are simulated.
32 devices in a mesh: mem: 8 (over z, x), grid: 4 (over y, core).
Axes of the slice: x: 2, y: 2, z: 4, core: 2. Of those that a mesh axis runs over, the one named last changes fastest.
Arguments:
- alpha: bfloat16 [16, 8, 768, 1536], P('mem', None, 'grid'), may hold values from -6 to 6
- perturbation: bfloat16 [16, 8, 768, 1536], P('mem', None, 'grid'), may hold values from -6 to 6
- legendre: bfloat16 [192, 128, 768], P('grid'), may hold values from -0.21875 to 0.21875
- response: float32 [192, 128], P('grid'), may hold values from 0.2 to 2
Outputs:
- increment: float32 [8, 768, 1536], P('mem', 'grid')
All inputs are finite; a program needn't handle non-finite values.
Results may differ from a plain program's by a relative error of at most 0.0063.
Values may be sent and summed in bfloat16 or wider, within the bound.
A program may use at most 128 MiB of HBM per device.

v0:
```python
import math
import jax
import jax.numpy as jnp
from jax import lax
from jax.sharding import PartitionSpec as P


def build_tables(lon_count, keep_dev, grid_count):
    col = jnp.arange(2 * keep_dev * grid_count, dtype=jnp.int32)
    block = col // (2 * keep_dev)
    part = col // keep_dev % 2
    wave = block * keep_dev + col % keep_dev
    lon = jnp.arange(lon_count, dtype=jnp.int32)
    phase = lon[:, None] * wave[None, :] % lon_count
    angle = phase.astype(jnp.float32) * jnp.float32(2.0 * math.pi / lon_count)
    basis = jnp.where(part[None, :] == 0, jnp.cos(angle), jnp.sin(angle))
    weight = jnp.where(wave == 0, jnp.float32(1.0), jnp.float32(2.0)) / jnp.float32(lon_count)
    forward = basis.astype(jnp.bfloat16)
    inverse = jnp.transpose(basis * weight[None, :]).astype(jnp.bfloat16)
    return (forward, inverse)


def legendre_filter(piece, legendre, response):
    cols, mem_dev, items, lat_count = piece.shape
    keep_dev = legendre.shape[0]
    split = piece.reshape(2, keep_dev, mem_dev, items, lat_count)
    coef = jnp.einsum("mnt,qmkit->qmkin", legendre, split, preferred_element_type=jnp.float32)
    coef = (coef * response[None, :, None, None, :]).astype(jnp.bfloat16)
    synth = jnp.einsum("mnt,qmkin->qmkit", legendre, coef, preferred_element_type=jnp.float32)
    return synth.astype(jnp.bfloat16).reshape(cols, mem_dev, items, lat_count)


def body(alpha, perturbation, legendre, response):
    mem_dev, levels, lat_dev, lon_count = alpha.shape
    keep_dev = legendre.shape[0]
    grid_count = lax.axis_size("grid")
    mem_count = lax.axis_size("mem")
    members = mem_dev * mem_count
    forward, inverse = build_tables(lon_count, keep_dev, grid_count)
    spectra = jnp.einsum("xc,klyx->ckly", forward, alpha, preferred_element_type=jnp.float32)
    spectra = spectra.astype(jnp.bfloat16)
    filtered = legendre_filter(
        lax.all_to_all(spectra, "grid", split_axis=0, concat_axis=3, tiled=True), legendre, response
    )
    returned = lax.all_to_all(filtered, "grid", split_axis=3, concat_axis=0, tiled=True)
    values = jnp.einsum("ckly,cx->klyx", returned, inverse, preferred_element_type=jnp.float32)
    total = lax.psum_scatter(
        jnp.sum(values * perturbation, axis=0), "mem", scatter_dimension=0, tiled=True
    )
    return total / jnp.sqrt(jnp.float32(members - 1))


def solution(mesh):
    placed = (
        P("mem", None, "grid", None),
        P("mem", None, "grid", None),
        P("grid", None, None),
        P("grid", None),
    )
    return jax.shard_map(
        body, mesh=mesh, in_specs=placed, out_specs=P("mem", "grid", None), check_vma=False
    )
```

profile of v0, /device:TPU:0, one launch (start us, length us, event | category | flops | bytes accessed | tf_op | source)
XLA Modules:
  0.0 337.0 jit_solution(17224794517558854112)
XLA Ops:
  6.6 17.5 %convolution_convert_fusion = bf16[384,2,8,192]{0,3,2,1:T(8,128)(2,1)} fusion(bf16[2,8,192,1536]{3,2,1,0:T(8,128)(2,1)} %param.4, s32[384]{0:T(512)S(1)} %fusion.57, pred[384]{0:T(512)(128)(4,1)S(1)} %fusion.59), kind=kOutput, calls=%fused_computation.25 | convolution fusion | flops 3631546368 | bytes 11798400 | tf_op jit(solution)/shard_map/xc,klyx->ckly/dot_general | solution.py:40
  24.1 4.0 %copy.15 = bf16[384,2,8,192]{3,2,1,0:T(8,128)(2,1)S(1)} copy(bf16[384,2,8,192]{0,3,2,1:T(8,128)(2,1)} %convolution_convert_fusion) | data formatting | bytes 4718592 | tf_op jit(solution)/shard_map/convert_element_type | solution.py:41
  28.1 41.0 %all_to_all.33 = bf16[384,2,8,192]{3,2,1,0:T(8,128)(2,1)S(1)} all-to-all(bf16[384,2,8,192]{3,2,1,0:T(8,128)(2,1)S(1)} %copy.15), channel_id=1, replica_groups=mesh['mem'=8,'grid'=4] {'grid'}, dimensions={0} | all-to-all | bytes 4718592 | tf_op jit(solution)/shard_map/all_to_all | solution.py:43
  69.1 4.0 %copy.40 = bf16[4,96,2,8,192]{4,0,3,2,1:T(4,128)(2,1)S(1)} copy(bf16[4,96,2,8,192]{4,3,2,1,0:T(8,128)(2,1)S(1)} %bitcast.48) | data formatting | bytes 4718592 | tf_op jit(solution)/shard_map/all_to_all | solution.py:43
  73.1 0.0 copy-start
  73.1 3.8 %reshape.57 = bf16[2,48,2,8,768]{4,3,2,1,0:T(8,128)(2,1)} reshape(bf16[96,2,8,4,192]{4,3,2,1,0:T(4,128)(2,1)S(1)} %bitcast.49) | data formatting | bytes 4718592 | tf_op jit(solution)/shard_map/reshape | solution.py:26
  76.9 0.0 copy-done
  76.9 11.5 %convert_bitcast_fusion = bf16[2,48,2,8,768]{4,3,2,0,1:T(8,128)(2,1)S(1)} fusion(bf16[48,128,768]{2,1,0:T(8,128)(2,1)} %param.6, bf16[2,48,2,8,768]{4,3,2,1,0:T(8,128)(2,1)} %reshape.57, f32[48,128]{1,0:T(8,128)S(1)} %copy-done), kind=kOutput, calls=%fused_computation.18 | convolution fusion | flops 605552640 | bytes 14180352 | tf_op jit(solution)/shard_map/mnt,qmkin->qmkit/dot_general | solution.py:29
  88.4 1.6 copy.18
  90.1 5.3 %copy.19 = bf16[96,2,8,768]{0,2,1,3:T(8,128)(2,1)} copy(bf16[96,2,8,768]{3,2,1,0:T(8,128)(2,1)} %bitcast.51) | data formatting | bytes 4718592 | tf_op jit(solution)/shard_map/reshape | solution.py:30
  95.4 3.7 %all-to-all-start.1 = ((bf16[96,2,8,768]{0,2,1,3:T(8,128)(2,1)}), bf16[96,2,8,768]{0,2,1,3:T(8,128)(2,1)S(1)}, u32[]{:S(2)}, u32[]{:S(2)}) async-start(bf16[96,2,8,768]{0,2,1,3:T(8,128)(2,1)} %copy.19), calls=%async_computation.1 | async-start | bytes 6291456 | tf_op jit(solution)/shard_map/all_to_all | solution.py:45
  99.1 0.3 reduce-scatter.2.cloned.1.call-start
  99.4 36.6 %all-to-all-done.1 = bf16[96,2,8,768]{0,2,1,3:T(8,128)(2,1)S(1)} async-done(((bf16[96,2,8,768]{0,2,1,3:T(8,128)(2,1)}), bf16[96,2,8,768]{0,2,1,3:T(8,128)(2,1)S(1)}, u32[]{:S(2)}, u32[]{:S(2)}) %all-to-all-start.1) | async-done | bytes 2359328 | tf_op jit(solution)/shard_map/all_to_all | solution.py:45
  135.9 4.1 %copy.39 = bf16[96,2,8,4,192]{0,3,4,2,1:T(4,128)(2,1)} copy(bf16[96,2,8,4,192]{0,2,1,4,3:T(8,128)(2,1)S(1)} %bitcast.47) | data formatting | bytes 4718592 | tf_op jit(solution)/shard_map/all_to_all | solution.py:45
  140.0 5.0 %all_to_all.30 = bf16[384,2,8,192]{0,3,2,1:T(8,128)(2,1)S(1)} reshape(bf16[4,96,2,8,192]{1,0,4,3,2:T(4,128)(2,1)} %bitcast.50) | data formatting | bytes 4718592 | tf_op jit(solution)/shard_map/all_to_all | solution.py:45
  145.0 20.1 %multiply_reduce_fusion = f32[8,192,1536]{2,1,0:T(8,128)} fusion(bf16[2,8,192,1536]{3,2,1,0:T(8,128)(2,1)} %param.5, bf16[384,2,8,192]{0,3,2,1:T(8,128)(2,1)S(1)} %all_to_all.30, f32[384]{0:T(512)S(1)} %select_multiply_fusion, s32[384]{0:T(512)S(1)} %fusion.57, pred[384]{0:T(512)(128)(4,1)S(1)} %fusion.59), kind=kOutput, calls=%fused_computation | convolution fusion | flops 3642753024 | bytes 21237120 | tf_op jit(solution)/shard_map/ckly,cx->klyx/dot_general | solution.py:46
  165.1 0.0 reduce-scatter.2.cloned.1.call-update
  165.2 162.6 %reduce-scatter.2.cloned.1.call-done = f32[1,192,1536]{2,1,0:T(8,128)} async-done(((f32[8,192,1536]{2,1,0:T(8,128)}), f32[1,192,1536]{2,1,0:T(8,128)}) %reduce-scatter.2.cloned.1.call-update) | async-done | bytes 1179664 | tf_op jit(solution)/shard_map/reduce_scatter | solution.py:47
  327.7 2.4 broadcast_multiply_fusion
  (3 shorter events, 0.0 us)
Async XLA Ops:
  73.1 3.8 %copy-start = (f32[48,128]{1,0:T(8,128)S(1)}, f32[48,128]{1,0:T(8,128)}, u32[]{:S(2)}) copy-start(f32[48,128]{1,0:T(8,128)} %param.7) | copy-start | bytes 73732
  95.4 40.6 %all-to-all-start.1 = ((bf16[96,2,8,768]{0,2,1,3:T(8,128)(2,1)}), bf16[96,2,8,768]{0,2,1,3:T(8,128)(2,1)S(1)}, u32[]{:S(2)}, u32[]{:S(2)}) async-start(bf16[96,2,8,768]{0,2,1,3:T(8,128)(2,1)} %copy.19), calls=%async_computation.1 | async-start | bytes 6291456 | tf_op jit(solution)/shard_map/all_to_all | solution.py:45
  99.1 228.7 %reduce-scatter.2.cloned.1.call-start = ((), (), s32[]{:S(2)}) async-start(), calls=%async_computation.3 | async-start | bytes 10616832 | tf_op jit(solution)/shard_map/reduce_scatter | solution.py:47
Sparse Core Ops, SparseCore 0:
  165.3 162.3 reduce-scatter.1
where the time goes:
time: 337 us
  waiting for transfers between devices  199 us (59%)
  matrix products  49.2 us (15%)
  blocking collectives  41 us (12%)
  local copies, waits for them, and re-layouts  27.8 us (8%)
  between operations  13.5 us (4%)
  starting transfers between devices  3.96 us (1%)
    reduce_scatter x1, waiting for transfers between devices, body(): lax.psum_scatter(jnp.sum(values * perturbation, axis=0), 'mem', scatter_d...  163 us
    all_to_all x1, blocking collectives, body(): lax.all_to_all(spectra, 'grid', split_axis=0, concat_axis=3, tiled=True)  41 us
    all_to_all x1, waiting for transfers between devices, body(): lax.all_to_all(filtered, 'grid', split_axis=3, concat_axis=0, tiled=True)  36.6 us
    dot_general x1, matrix products, body(): jnp.einsum('ckly,cx->klyx', returned, inverse, preferred_element_type=jnp...  20.1 us
    dot_general x1, matrix products, body(): jnp.einsum('xc,klyx->ckly', forward, alpha, preferred_element_type=jnp.fl...  17.5 us
    dot_general x1, matrix products, legendre_filter(): jnp.einsum('mnt,qmkin->qmkit', legendre, coef, preferred_element_type=jnp...  11.5 us
    all_to_all x2, local copies, waits for them, and re-layouts, body(): lax.all_to_all(filtered, 'grid', split_axis=3, concat_axis=0, tiled=True)  9.05 us
  transfers between devices with their start and end apart: 2, of which 2 were waited for; matrix products, arithmetic and copies ran while one was open for 0% of the time, Pallas kernels for 0%

commit v1 on v0

--- a/solution.py
+++ b/solution.py
@@ -3,6 +3,36 @@
 import jax.numpy as jnp
 from jax import lax
 from jax.sharding import PartitionSpec as P
+
+
+def _work_circles(message, row_dim, u):
+    tile_out, mixed_arr = (message.shape[:row_dim], message.shape[row_dim + 1 :])
+    return jnp.moveaxis(message.reshape(*tile_out, u, -1, *mixed_arr), row_dim, 0)
+
+
+def indices_compute(target, on_dim):
+    target = jnp.moveaxis(target, 0, on_dim)
+    t1 = target.shape
+    return target.reshape(*t1[:on_dim], t1[on_dim] * t1[on_dim + 1], *t1[on_dim + 2 :])
+
+
+def squares_read(s0, shard_axis, frame, xs):
+    all_rows = jax.lax.psum(1, axis_name=shard_axis)
+    field_out = jax.lax.axis_index(shard_axis)
+    local_now, block_next = (all_rows, field_out)
+    formed = _work_circles(s0, frame, local_now)
+    block_list = [formed[block_next]]
+    for m in range(1, local_now):
+        w2 = formed[(block_next + m) % local_now]
+        block_list.append(
+            jax.lax.ppermute(
+                w2,
+                axis_name=shard_axis,
+                perm=[(kk, (kk + m) % local_now) for kk in range(local_now)],
+            )
+        )
+    formed = jnp.stack(block_list)[(block_next - jnp.arange(local_now)) % local_now]
+    return indices_compute(formed, xs)
 
 
 def build_tables(lon_count, keep_dev, grid_count):
@@ -39,9 +69,7 @@
     forward, inverse = build_tables(lon_count, keep_dev, grid_count)
     spectra = jnp.einsum("xc,klyx->ckly", forward, alpha, preferred_element_type=jnp.float32)
     spectra = spectra.astype(jnp.bfloat16)
-    filtered = legendre_filter(
-        lax.all_to_all(spectra, "grid", split_axis=0, concat_axis=3, tiled=True), legendre, response
-    )
+    filtered = legendre_filter(squares_read(spectra, "grid", 0, 3), legendre, response)
     returned = lax.all_to_all(filtered, "grid", split_axis=3, concat_axis=0, tiled=True)
     values = jnp.einsum("ckly,cx->klyx", returned, inverse, preferred_element_type=jnp.float32)
     total = lax.psum_scatter(

time: 337 us -> 340 us (level)
  blocking collectives: 41 us -> 0 us
  waiting for transfers between devices: 199 us -> 234 us
  local copies, waits for them, and re-layouts: 27.8 us -> 32.3 us
    all_to_all x1 -> x0, blocking collectives: 41 us -> none  [body(): lax.all_to_all(spectra, 'grid', split_axis=0, concat_axis=3, tiled=True)]
    ppermute x0 -> x3, waiting for transfers between devices: none -> 34.8 us  [squares_read(): jax.lax.ppermute(w2, axis_name=shard_axis, perm=[(kk, (kk + m) % local_no...]
    transpose x0 -> x1, local copies, waits for them, and re-layouts: none -> 5.94 us  [indices_compute(): target = jnp.moveaxis(target, 0, on_dim)]
    all_to_all x1 -> x0, local copies, waits for them, and re-layouts: 4.05 us -> none  [body(): lax.all_to_all(spectra, 'grid', split_axis=0, concat_axis=3, tiled=True)]
    convert_element_type x1 -> x0, local copies, waits for them, and re-layouts: 4.03 us -> none  [body(): spectra = spectra.astype(jnp.bfloat16)]
    another operation x0 -> x1, local copies, waits for them, and re-layouts: none -> 3.8 us  [legendre_filter(): split = piece.reshape(2, keep_dev, mem_dev, items, lat_count)]
  transfers between devices with their start and end apart: 2 -> 5, of which waited for: 2 -> 4; matrix products, arithmetic and copies ran while one was open for 0% -> 0% of each run, Pallas kernels for 0% -> 0%
where the time goes in v1:
time: 340 us
  waiting for transfers between devices  234 us (69%)
  matrix products  49.2 us (14%)
  local copies, waits for them, and re-layouts  32.3 us (9%)
  between operations  13.5 us (4%)
  starting transfers between devices  7.23 us (2%)
    reduce_scatter x1, waiting for transfers between devices, body(): lax.psum_scatter(jnp.sum(values * perturbation, axis=0), 'mem', scatter_d...  163 us
    all_to_all x1, waiting for transfers between devices, body(): lax.all_to_all(filtered, 'grid', split_axis=3, concat_axis=0, tiled=True)  36.6 us
    ppermute x3, waiting for transfers between devices, squares_read(): jax.lax.ppermute(w2, axis_name=shard_axis, perm=[(kk, (kk + m) % local_no...  34.8 us
    dot_general x1, matrix products, body(): jnp.einsum('ckly,cx->klyx', returned, inverse, preferred_element_type=jnp...  20.1 us
    dot_general x1, matrix products, body(): jnp.einsum('xc,klyx->ckly', forward, alpha, preferred_element_type=jnp.fl...  17.5 us
    dot_general x1, matrix products, legendre_filter(): jnp.einsum('mnt,qmkin->qmkit', legendre, coef, preferred_element_type=jnp...  11.6 us
    all_to_all x2, local copies, waits for them, and re-layouts, body(): lax.all_to_all(filtered, 'grid', split_axis=3, concat_axis=0, tiled=True)  9.03 us
  transfers between devices with their start and end apart: 5, of which 4 were waited for; matrix products, arithmetic and copies ran while one was open for 0% of the time, Pallas kernels for 0%

profile of v1, /device:TPU:0, one launch (start us, length us, event | category | flops | bytes accessed | tf_op | source)
XLA Modules:
  0.0 339.7 jit_solution(325998615780174811)
XLA Ops:
  6.6 17.5 %convolution_convert_fusion = bf16[384,2,8,192]{0,3,2,1:T(8,128)(2,1)} fusion(bf16[2,8,192,1536]{3,2,1,0:T(8,128)(2,1)} %param.4, s32[384]{0:T(512)S(1)} %fusion.57, pred[384]{0:T(512)(128)(4,1)S(1)} %fusion.59), kind=kOutput, calls=%fused_computation.26 | convolution fusion | flops 3631546368 | bytes 11798400 | tf_op jit(solution)/shard_map/xc,klyx->ckly/dot_general | solution.py:70
  24.1 4.0 %copy.37 = bf16[384,2,8,192]{3,2,1,0:T(8,128)(2,1)S(1)} copy(bf16[384,2,8,192]{0,3,2,1:T(8,128)(2,1)} %convolution_convert_fusion) | data formatting | bytes 4718592 | tf_op jit(solution)/shard_map/reshape | solution.py:10
  28.1 0.2 constant_dynamic-slice_fusion
  28.3 2.5 collective-permute-start.2
  30.8 0.6 collective-permute-start.1
  31.5 0.2 collective-permute-start
  31.6 17.0 %collective-permute-done.2 = bf16[96,2,8,192]{3,2,1,0:T(8,128)(2,1)S(1)} collective-permute-done((bf16[96,2,8,192]{3,2,1,0:T(8,128)(2,1)S(1)}, bf16[96,2,8,192]{3,2,1,0:T(8,128)(2,1)S(1)}, u32[]{:S(2)}, u32[]{:S(2)}) %collective-permute-start.2) | collective-permute-done | bytes 589856 | tf_op jit(solution)/shard_map/ppermute | solution.py:28
  48.7 17.8 %collective-permute-done.1 = bf16[96,2,8,192]{3,2,1,0:T(8,128)(2,1)S(1)} collective-permute-done((bf16[96,2,8,192]{3,2,1,0:T(8,128)(2,1)S(1)}, bf16[96,2,8,192]{3,2,1,0:T(8,128)(2,1)S(1)}, u32[]{:S(2)}, u32[]{:S(2)}) %collective-permute-start.1) | collective-permute-done | bytes 589856 | tf_op jit(solution)/shard_map/ppermute | solution.py:28
  66.5 0.0 collective-permute-done
  66.5 0.8 pad_maximum_fusion
  67.3 2.4 gather_fusion
  69.7 5.9 %copy.26 = bf16[96,2,8,4,192]{4,3,2,1,0:T(4,128)(2,1)S(1)} copy(bf16[96,2,8,4,192]{4,2,1,0,3:T(8,128)(2,1)} %bitcast.57) | data formatting | bytes 4718592 | tf_op jit(solution)/shard_map/transpose | solution.py:14
  75.6 0.0 copy-start
  75.6 3.8 %reshape_reshape.3 = bf16[2,48,2,8,768]{4,3,2,1,0:T(8,128)(2,1)} reshape(bf16[96,2,8,4,192]{4,3,2,1,0:T(4,128)(2,1)S(1)} %copy.26) | data formatting | bytes 4718592 | tf_op jit(solution)/shard_map/reshape;reshape | solution.py:56
  79.4 0.0 copy-done
  79.4 11.6 %convert_bitcast_fusion = bf16[2,48,2,8,768]{4,3,2,0,1:T(8,128)(2,1)S(1)} fusion(bf16[48,128,768]{2,1,0:T(8,128)(2,1)} %param.6, bf16[2,48,2,8,768]{4,3,2,1,0:T(8,128)(2,1)} %reshape_reshape.3, f32[48,128]{1,0:T(8,128)S(1)} %copy-done), kind=kOutput, calls=%fused_computation.19 | convolution fusion | flops 605552640 | bytes 14180352 | tf_op jit(solution)/shard_map/mnt,qmkin->qmkit/dot_general | solution.py:59
  91.1 1.6 copy.28
  92.7 5.3 %copy.29 = bf16[96,2,8,768]{0,2,1,3:T(8,128)(2,1)} copy(bf16[96,2,8,768]{3,2,1,0:T(8,128)(2,1)} %bitcast.60) | data formatting | bytes 4718592 | tf_op jit(solution)/shard_map/reshape | solution.py:60
  98.0 3.7 %all-to-all-start = ((bf16[96,2,8,768]{0,2,1,3:T(8,128)(2,1)}), bf16[96,2,8,768]{0,2,1,3:T(8,128)(2,1)S(1)}, u32[]{:S(2)}, u32[]{:S(2)}) async-start(bf16[96,2,8,768]{0,2,1,3:T(8,128)(2,1)} %copy.29), calls=%async_computation | async-start | bytes 6291456 | tf_op jit(solution)/shard_map/all_to_all | solution.py:73
  101.7 0.3 reduce-scatter.2.cloned.1.call-start
  102.0 36.6 %all-to-all-done = bf16[96,2,8,768]{0,2,1,3:T(8,128)(2,1)S(1)} async-done(((bf16[96,2,8,768]{0,2,1,3:T(8,128)(2,1)}), bf16[96,2,8,768]{0,2,1,3:T(8,128)(2,1)S(1)}, u32[]{:S(2)}, u32[]{:S(2)}) %all-to-all-start) | async-done | bytes 2359328 | tf_op jit(solution)/shard_map/all_to_all | solution.py:73
  138.6 4.1 %copy.49 = bf16[96,2,8,4,192]{0,3,4,2,1:T(4,128)(2,1)} copy(bf16[96,2,8,4,192]{0,2,1,4,3:T(8,128)(2,1)S(1)} %bitcast.56) | data formatting | bytes 4718592 | tf_op jit(solution)/shard_map/all_to_all | solution.py:73
  142.6 5.0 %all_to_all.16 = bf16[384,2,8,192]{0,3,2,1:T(8,128)(2,1)S(1)} reshape(bf16[4,96,2,8,192]{1,0,4,3,2:T(4,128)(2,1)} %bitcast.59) | data formatting | bytes 4718592 | tf_op jit(solution)/shard_map/all_to_all | solution.py:73
  147.6 20.1 %multiply_reduce_fusion = f32[8,192,1536]{2,1,0:T(8,128)} fusion(bf16[2,8,192,1536]{3,2,1,0:T(8,128)(2,1)} %param.5, bf16[384,2,8,192]{0,3,2,1:T(8,128)(2,1)S(1)} %all_to_all.16, f32[384]{0:T(512)S(1)} %select_multiply_fusion, s32[384]{0:T(512)S(1)} %fusion.57, pred[384]{0:T(512)(128)(4,1)S(1)} %fusion.59), kind=kOutput, calls=%fused_computation.1 | convolution fusion | flops 3642753024 | bytes 21237120 | tf_op jit(solution)/shard_map/ckly,cx->klyx/dot_general | solution.py:74
  167.7 0.0 reduce-scatter.2.cloned.1.call-update
  167.8 162.7 %reduce-scatter.2.cloned.1.call-done = f32[1,192,1536]{2,1,0:T(8,128)} async-done(((f32[8,192,1536]{2,1,0:T(8,128)}), f32[1,192,1536]{2,1,0:T(8,128)}) %reduce-scatter.2.cloned.1.call-update) | async-done | bytes 1179664 | tf_op jit(solution)/shard_map/reduce_scatter | solution.py:75
  330.5 2.4 broadcast_multiply_fusion
  (5 shorter events, 0.1 us)
Async XLA Ops:
  28.3 20.3 %collective-permute-start.2 = (bf16[96,2,8,192]{3,2,1,0:T(8,128)(2,1)S(1)}, bf16[96,2,8,192]{3,2,1,0:T(8,128)(2,1)S(1)}, u32[]{:S(2)}, u32[]{:S(2)}) collective-permute-start(bf16[96,2,8,192]{3,2,1,0:T(8,128)(2,1)S(1)} %get-tuple-element.6), channel_id=1, source_target_pairs={{0,3},{1,0},{2,1},{3,2},{4,7},{5,4},{6,5},{7,6},{8,11},{9,8},{10,9... | collective-permute-start | bytes 1769480 | tf_op jit(solution)/shard_map/ppermute | solution.py:28
  30.8 35.6 %collective-permute-start.1 = (bf16[96,2,8,192]{3,2,1,0:T(8,128)(2,1)S(1)}, bf16[96,2,8,192]{3,2,1,0:T(8,128)(2,1)S(1)}, u32[]{:S(2)}, u32[]{:S(2)}) collective-permute-start(bf16[96,2,8,192]{3,2,1,0:T(8,128)(2,1)S(1)} %get-tuple-element.7), channel_id=1, source_target_pairs={{0,2},{1,3},{2,0},{3,1},{4,6},{5,7},{6,4},{7,5},{8,10},{9,11},{10,... | collective-permute-start | bytes 1769480 | tf_op jit(solution)/shard_map/ppermute | solution.py:28
  31.5 35.0 %collective-permute-start = (bf16[96,2,8,192]{3,2,1,0:T(8,128)(2,1)S(1)}, bf16[96,2,8,192]{3,2,1,0:T(8,128)(2,1)S(1)}, u32[]{:S(2)}, u32[]{:S(2)}) collective-permute-start(bf16[96,2,8,192]{3,2,1,0:T(8,128)(2,1)S(1)} %get-tuple-element.8), channel_id=1, source_target_pairs={{0,1},{1,2},{2,3},{3,0},{4,5},{5,6},{6,7},{7,4},{8,9},{9,10},{10,1... | collective-permute-start | bytes 1769480 | tf_op jit(solution)/shard_map/ppermute | solution.py:28
  75.6 3.8 %copy-start = (f32[48,128]{1,0:T(8,128)S(1)}, f32[48,128]{1,0:T(8,128)}, u32[]{:S(2)}) copy-start(f32[48,128]{1,0:T(8,128)} %param.7) | copy-start | bytes 73732
  98.0 40.6 %all-to-all-start = ((bf16[96,2,8,768]{0,2,1,3:T(8,128)(2,1)}), bf16[96,2,8,768]{0,2,1,3:T(8,128)(2,1)S(1)}, u32[]{:S(2)}, u32[]{:S(2)}) async-start(bf16[96,2,8,768]{0,2,1,3:T(8,128)(2,1)} %copy.29), calls=%async_computation | async-start | bytes 6291456 | tf_op jit(solution)/shard_map/all_to_all | solution.py:73
  101.7 228.8 %reduce-scatter.2.cloned.1.call-start = ((), (), s32[]{:S(2)}) async-start(), calls=%async_computation.2 | async-start | bytes 10616832 | tf_op jit(solution)/shard_map/reduce_scatter | solution.py:75
Sparse Core Ops, SparseCore 0:
  167.9 162.5 reduce-scatter.1
